TPU v7x, 16 devices: a 4x2x1 block of a 4x4x8 slice. The times are simulated.
16 devices in a mesh: rep: 2 (over y, z), seq: 8 (over x, core).
Axes of the slice: x: 4, y: 2, z: 1, core: 2. Of those that a mesh axis runs over, the one named last changes fastest.
The devices are a block of a 4x4x8 slice.
Arguments:
- hidden: bfloat16 [128, 4096], P('rep'), parts along dimension 0
- w_query: bfloat16 [4096, 4096], replicated
- w_key: bfloat16 [4096, 1024], replicated
- w_value: bfloat16 [4096, 1024], replicated
- w_out: bfloat16 [4096, 4096], P('seq')
- k_cache: bfloat16 [128, 1024, 8, 128], P('rep', 'seq'), parts along dimension 0
- v_cache: bfloat16 [128, 1024, 8, 128], P('rep', 'seq'), parts along dimension 0
- positions: int32 [128], P('rep'), parts along dimension 0
Outputs:
- output 1: bfloat16 [128, 4096], P('rep'), parts along dimension 0
- output 2: bfloat16 [128, 1024, 8, 128], P('rep', 'seq'), parts along dimension 0
- output 3: bfloat16 [128, 1024, 8, 128], P('rep', 'seq'), parts along dimension 0
There are 2 independent parts. A program takes and returns all parts, laid end to end along the dimension named above; an argument that names none is the same for every part.
All inputs are finite; a program needn't handle non-finite values.
Results may differ from a plain program's by a relative error of at most 0.00593277.
Values are sent between devices in bfloat16 or wider.
A program may use at most 768 MiB of HBM per device.

v0:
```python
import functools
import math

import jax
import jax.numpy as jnp
from jax import lax
from jax.experimental import pallas as pl
from jax.experimental.pallas import tpu as pltpu
from jax.sharding import PartitionSpec as P

MESH = pl.DeviceIdType.MESH
NEG = -3.4028234e38
F32, BF16 = jnp.float32, jnp.bfloat16
CORES = 2
NT = (((1,), (1,)), ((), ()))


def step_kernel(chips, x_hbm, wq_hbm, wk_hbm, wv_hbm, wo_hbm, k_hbm, v_hbm, pos_ref,
                yfull, kout, vout, rows_ref,
                x_v, wbuf, wo_v, qs, q_all, kv_all, sa, sb, mt_ref, pos2_ref, oraw, mraw, lraw, om, op, orecv,
                ys, yp, yr,
                lsem, kvsem, q_ss, q_rs, n_ss, n_rs, od_s, od_r, oi_s, oi_r, yd_s, yd_r, yi_s, yi_r, ag_s, ag_r):
    batch = k_hbm.shape[0]
    local_len = k_hbm.shape[1] // 8
    chunks = om.shape[0]
    cb = batch // chunks
    half = batch // 2
    scale2 = k_hbm.shape[2] ** -0.5 * math.log2(math.e)
    rep = lax.axis_index('rep')
    me = lax.axis_index('seq')
    chip, core = me // CORES, me % CORES
    base = me * local_len
    quarter = (chip % 2) * CORES + core

    def dev(c, e):
        return (rep, lax.rem(c, chips) * CORES + e)

    partner = dev(chip, 1 - core)
    ncols = 256
    lx = pltpu.make_async_copy(x_hbm, x_v, lsem.at[0])
    hd = wbuf.shape[1] // 2
    lw = [[pltpu.make_async_copy(wq_hbm.at[pl.ds(n * hd, hd), pl.ds(pl.multiple_of(quarter * 1024 + i * 512, 512), 512)],
                                 wbuf.at[i, pl.ds(n * hd, hd)], lsem.at[1 + i * 2 + n]) for n in range(2)] for i in range(2)]
    lk = pltpu.make_async_copy(wk_hbm.at[:, pl.ds(pl.multiple_of(quarter * ncols, ncols), ncols)], wbuf.at[2, :, pl.ds(0, ncols)], lsem.at[5])
    lv = pltpu.make_async_copy(wv_hbm.at[:, pl.ds(pl.multiple_of(quarter * ncols, ncols), ncols)], wbuf.at[2, :, pl.ds(ncols, ncols)], lsem.at[6])
    lo = pltpu.make_async_copy(wo_hbm, wo_v, lsem.at[7])
    lkc = [pltpu.make_async_copy(k_hbm.at[pl.ds(i * cb, cb)], kout.at[pl.ds(i * cb, cb)], kvsem.at[0, i]) for i in range(chunks)]
    lvc = [pltpu.make_async_copy(v_hbm.at[pl.ds(i * cb, cb)], vout.at[pl.ds(i * cb, cb)], kvsem.at[1, i]) for i in range(chunks)]
    lx.start()
    for i in range(2):
        for n in range(2):
            lw[i][n].start()

    barrier = pltpu.get_barrier_semaphore()
    for d in range(chips):
        for f in range(CORES):
            if d or f:
                pl.semaphore_signal(barrier, inc=1, device_id=dev(chip + d, lax.rem(core + f, CORES)), device_id_type=MESH)

    lane_b = (lax.broadcasted_iota(jnp.int32, pos2_ref.shape, 1) + lax.broadcasted_iota(jnp.int32, pos2_ref.shape, 0) * pos2_ref.shape[1]) // 2
    pv = jnp.zeros(pos2_ref.shape, jnp.int32)
    for b in range(batch):
        pv = jnp.where(lane_b == b, pos_ref[b], pv)
    pos2_ref[...] = pv

    lx.wait()
    for i in range(2):
        lw[i][0].wait()
        q = jnp.dot(x_v[:, :hd], wbuf[i, :hd], preferred_element_type=F32)
        lw[i][1].wait()
        if i == 0:
            lk.start()
            lv.start()
        q = q + jnp.dot(x_v[:, hd:], wbuf[i, hd:], preferred_element_type=F32)
        for h in range(4):
            qs[pl.ds(i * 4 + h, batch, stride=8), :] = q[:, h * 128:(h + 1) * 128]
    q_all[quarter] = qs[...].astype(BF16)
    pl.semaphore_wait(barrier, chips * CORES - 1)

    def spread(buf, rows, ss, rs):
        copies = [pltpu.make_async_remote_copy(buf.at[quarter], buf.at[quarter], ss.at[0], rs.at[0], device_id=partner, device_id_type=MESH)]
        for side, shift in ((0, 1), (1, chips - 1)):
            part = pl.ds(side * rows // 2, rows // 2)
            copies.append(pltpu.make_async_remote_copy(
                buf.at[quarter, part], buf.at[quarter, part], ss.at[1 + side], rs.at[1 + side], device_id=dev(chip + shift, core), device_id_type=MESH))
        return copies

    def hand_on(copies, buf, rows, ss, rs):
        other = ((chip + 1) % 2) * CORES + core
        for side in range(2):
            copies[1 + side].wait_recv()
            part = pl.ds(side * rows // 2, rows // 2)
            c = pltpu.make_async_remote_copy(buf.at[other, part], buf.at[other, part], ss.at[3 + side], rs.at[3 + side], device_id=partner, device_id_type=MESH)
            c.start()
            copies.append(c)

    def arrive(copies):
        copies[0].wait_recv()
        copies[3].wait_recv()
        copies[4].wait_recv()

    q_copies = spread(q_all, batch * 8, q_ss, q_rs)
    for c in q_copies:
        c.start()
    lkc[0].start()
    lvc[0].start()
    lk.wait()
    lv.wait()
    kv = jnp.dot(x_v[...], wbuf[2], preferred_element_type=F32)
    for w in range(2):
        for k in range(2):
            qs[pl.ds(w * 128 + k, batch, stride=2), :] = kv[:, w * 256 + k * 128:w * 256 + (k + 1) * 128]
    for hf in range(2):
        for w in range(2):
            kv_all[quarter, hf * 128 + w * 64:hf * 128 + w * 64 + 64, :] = qs[w * 128 + hf * 64:w * 128 + hf * 64 + 64, :].astype(BF16)
    n_copies = spread(kv_all, batch * 4, n_ss, n_rs)
    for c in n_copies:
        c.start()
    rowb = lax.broadcasted_iota(jnp.int32, (64, 128), 0) // 8 % 2
    bm0 = jnp.where(rowb == 0, 1.0, 0.0).astype(BF16)
    bm1 = jnp.where(rowb == 1, 1.0, 0.0).astype(BF16)

    hand_on(q_copies, q_all, batch * 8, q_ss, q_rs)
    for i in range(1, chunks):
        lkc[i].start()
        lvc[i].start()
    lo.start()
    hand_on(n_copies, kv_all, batch * 4, n_ss, n_rs)
    arrive(q_copies)

    qlane = lax.broadcasted_iota(jnp.int32, (8, 128), 1)
    own_head = lax.broadcasted_iota(jnp.int32, (8, 128), 0) == (qlane % 64) // 16 * 2 + (qlane % 8) // 4
    qseq = qlane // 64 * 2 + (qlane // 8) % 2
    mt_ref[...] = jnp.zeros_like(mt_ref)

    def scores(qi, buf):
        zero = jnp.zeros((64, 256), BF16)
        rows = []
        for ph in range(2):
            p0 = (2 * qi + ph) * 16
            q = jnp.concatenate([q_all[t, p0:p0 + 16, :] for t in range(4)], axis=0)
            blocks = [q * bm0, q * bm1]
            rows.append(jnp.concatenate(blocks + [zero] if ph == 0 else [zero] + blocks, axis=1))
        kc = jnp.concatenate([kout[4 * qi + j] for j in range(4)], axis=1)
        s = lax.dot_general(kc, jnp.concatenate(rows, axis=0), NT, preferred_element_type=F32).reshape(local_len, 8, 128)
        lim = jnp.full((8, 128), -1, jnp.int32)
        for j in range(4):
            lim = jnp.where(own_head & (qseq == j), pos_ref[4 * qi + j] - base, lim)
        s = jnp.where(lax.broadcasted_iota(jnp.int32, s.shape, 0) < lim[None], s, -jnp.inf)
        buf[...] = s.reshape(buf.shape)
        return jnp.maximum(jnp.max(jnp.max(s, axis=0), axis=0, keepdims=True), NEG)

    def weigh(qi, buf, m):
        p = jnp.exp2((buf[...] - m) * scale2)
        quad = qi % (cb // 4)
        mt_ref[0, quad:quad + 1, :] = m
        mt_ref[1, quad:quad + 1, :] = jnp.sum(p, axis=0, keepdims=True)
        pt = p.astype(BF16).T
        for ph in range(2):
            b0 = 4 * qi + 2 * ph
            vc = jnp.concatenate([vout[b0], vout[b0 + 1]], axis=1)
            o = jnp.dot(pt[ph * 64:(ph + 1) * 64, :], vc, preferred_element_type=F32)
            for t in range(4):
                for b in range(2):
                    r0 = (b0 % cb + b) * 8
                    oraw[t, r0:r0 + 8, :] = o[t * 16 + b * 8:t * 16 + b * 8 + 8, b * 128:(b + 1) * 128]

    rows_c = cb * 8
    carry = {}

    def attend(k):
        if k == 0:
            lkc[0].wait()
            carry['m'] = scores(0, sa)
        elif k % 2 == 1 and k < 2 * chunks - 1:
            lkc[(k + 1) // 2].wait()
        if k % 2 == 0:
            lvc[k // 2].wait()
        m_b = scores(2 * k + 1, sb)
        weigh(2 * k, sa, carry['m'])
        if k < 2 * chunks - 1:
            carry['m'] = scores(2 * k + 2, sa)
        weigh(2 * k + 1, sb, m_b)

    lane = lax.broadcasted_iota(jnp.int32, (8, 128), 1)
    od, oi, yd, yi, ag = {}, {}, {}, {}, {}

    def finalize(i):
        hf = i * cb // half
        first = i * rows_c - hf * half * 8
        rr = lax.broadcasted_iota(jnp.int32, (rows_c, 64), 0) + first
        cc = lax.broadcasted_iota(jnp.int32, (rows_c, 64), 1)
        rel = pos2_ref[hf:hf + 1, :] - base
        keep = (rr // 4 == cc) & (rel >= 0) & (rel < local_len)
        mt, lt = mt_ref[0].T, mt_ref[1].T

        def by_row(x, t):
            return jnp.concatenate([jnp.broadcast_to(x[(p % 2) * 64 + t * 16:(p % 2) * 64 + t * 16 + 16, p // 2:p // 2 + 1], (16, 128))
                                    for p in range(cb // 2)], axis=0)

        quarters = range(4)
        sn = [lax.dot_general(q_all[t, i * rows_c:(i + 1) * rows_c, :], kv_all[t, hf * 128:hf * 128 + 64, :], NT, preferred_element_type=F32) for t in quarters]
        mo = [by_row(mt, t) for t in quarters]
        lo_ = [by_row(lt, t) for t in quarters]
        sn = [jnp.where(keep, x, -jnp.inf) for x in sn]
        top = [jnp.max(x, axis=1, keepdims=True) for x in sn]
        mn = [jnp.maximum(x, y) for x, y in zip(mo, top)]
        pn = [jnp.exp2((x - y[:, :64]) * scale2) for x, y in zip(sn, mn)]
        on = [jnp.dot(pn[t].astype(BF16), kv_all[t, hf * 128 + 64:hf * 128 + 128, :], preferred_element_type=F32) for t in quarters]
        ln = [jnp.sum(x, axis=1, keepdims=True) for x in pn]
        for t in quarters:
            w = jnp.exp2((mo[t] - mn[t]) * scale2)
            mraw[t] = mn[t]
            lraw[t] = lo_[t] * w + ln[t]
            oraw[t] = oraw[t] * w + on[t]
        for e in range(CORES):
            for t in range(4):
                mp = jnp.zeros((8, 128), F32)
                lp = jnp.zeros((8, 128), F32)
                for h in range(4):
                    src = pl.ds(e * 4 + h, cb, stride=8)
                    om[i, e, t, h * cb:(h + 1) * cb, :] = oraw[t, src, :]
                    mh = mraw[t, src, :]
                    lh = lraw[t, src, :]
                    for g in range(cb // 8):
                        sel = lane == h * (cb // 8) + g
                        mp = jnp.where(sel, mh[g * 8:(g + 1) * 8], mp)
                        lp = jnp.where(sel, lh[g * 8:(g + 1) * 8], lp)
                om[i, e, t, cb * 4:cb * 4 + 8, :] = mp
                om[i, e, t, cb * 4 + 8:cb * 4 + 16, :] = lp
        od[i] = pltpu.make_async_remote_copy(om.at[i, 1 - core], op.at[i], od_s.at[i], od_r.at[i], device_id=partner, device_id_type=MESH)
        od[i].start()

    nrow = cb * 4

    def merge(parts):
        ms = [p[nrow:nrow + 8] for p in parts]
        m = functools.reduce(jnp.maximum, ms)
        ws = [jnp.exp2((x - m) * scale2) for x in ms]
        l = functools.reduce(jnp.add, [w * p[nrow + 8:nrow + 16] for w, p in zip(ws, parts)])
        return m, l, ws

    def chip_reduce(i):
        od[i].wait_recv()
        for t in range(4):
            fold(om.at[i, core, t], om[i, core, t], op[i, t])
        oi[i] = []
        for d in range(1, chips):
            c = pltpu.make_async_remote_copy(om.at[i, core, lax.rem(chip + d, chips)], orecv.at[i, d - 1], oi_s.at[i, d - 1], oi_r.at[i, d - 1],
                                             device_id=dev(chip + d, core), device_id_type=MESH)
            c.start()
            oi[i].append(c)

    def fold(dst, a, b):
        m, l, (wa, wb) = merge([a, b])
        for g in range(nrow // 8):
            r = slice(g * 8, g * 8 + 8)
            dst[g * 8:g * 8 + 8, :] = a[r] * wa[:, g:g + 1] + b[r] * wb[:, g:g + 1]
        dst[nrow:nrow + 8, :] = m
        dst[nrow + 8:nrow + 16, :] = l

    def project(i):
        for c in oi[i]:
            c.wait_recv()
        if i == 0:
            lo.wait()
        parts = [om[i, core, chip]] + [orecv[i, d] for d in range(chips - 1)]
        m, l, ws = merge(parts)
        rl = 1.0 / l
        heads = []
        for h in range(4):
            rows = []
            for g in range(h * (cb // 8), (h + 1) * (cb // 8)):
                o = functools.reduce(jnp.add, [p[g * 8:g * 8 + 8] * w[:, g:g + 1] for p, w in zip(parts, ws)])
                rows.append(o * rl[:, g:g + 1])
            heads.append(jnp.concatenate(rows, axis=0).astype(BF16))
        lhs = jnp.concatenate(heads, axis=1)
        for e in range(CORES):
            for t in range(4):
                c0 = (e * 4 + t) * 512
                ys[i, e, t] = jnp.dot(lhs, wo_v[:, c0:c0 + 512], preferred_element_type=F32)
        yd[i] = pltpu.make_async_remote_copy(ys.at[i, 1 - core], yp.at[i], yd_s.at[i], yd_r.at[i], device_id=partner, device_id_type=MESH)
        yd[i].start()

    def y_chip(i):
        yd[i].wait_recv()
        ys[i, core] = ys[i, core] + yp[i]
        yi[i] = []
        for d in range(1, chips):
            c = pltpu.make_async_remote_copy(ys.at[i, core, lax.rem(chip + d, chips)], yr.at[i, d - 1], yi_s.at[i, d - 1], yi_r.at[i, d - 1],
                                             device_id=dev(chip + d, core), device_id_type=MESH)
            c.start()
            yi[i].append(c)

    def block(i, c):
        return (pl.ds(i * cb, cb), pl.ds(pl.multiple_of((core * 4 + c) * 512, 512), 512))

    def lay_rows():
        for w in range(2):
            for t in range(4):
                for hf in range(2):
                    sa[:64, :] = kv_all[t, hf * 128 + w * 64:hf * 128 + w * 64 + 64, :].astype(F32)
                    for k in range(2):
                        qs[pl.ds(hf * half * 8 + t * 2 + k, half, stride=8), :] = sa[pl.ds(k, half, stride=2), :]
            rows_ref[w] = qs[...].astype(BF16)

    def y_final(i):
        if i == chunks - 1:
            lay_rows()
        for c in yi[i]:
            c.wait_recv()
        y = ys[i, core, chip]
        for d in range(chips - 1):
            y = y + yr[i, d]
        yfull[block(i, chip)] = y.astype(BF16)
        ag[i] = []
        if i == chunks - 1:
            for d in range(chips):
                for f in range(CORES):
                    if d or f:
                        push(i, chip, dev(chip + d, lax.rem(core + f, CORES)))
        else:
            for d in range(1, chips):
                push(i, chip, dev(chip + d, core))
            push(i, chip, partner)

    def push(i, c, target):
        slot = len(ag[i])
        cp = pltpu.make_async_remote_copy(yfull.at[block(i, c)], yfull.at[block(i, c)], ag_s.at[i, slot], ag_r.at[i, slot], device_id=target, device_id_type=MESH)
        cp.start()
        ag[i].append(cp)

    def pass_on(i):
        for d in range(1, chips):
            ag[i][d - 1].wait_recv()
            push(i, lax.rem(chip + chips - d, chips), partner)

    plan = {1: [(finalize, 0)], 2: [(chip_reduce, 0)], 3: [(finalize, 1)], 4: [(chip_reduce, 1)],
            5: [(finalize, 2), (project, 0)], 6: [(chip_reduce, 2), (y_chip, 0), (project, 1)],
            7: [(finalize, 3), (y_chip, 1), (chip_reduce, 3), (y_final, 0), (project, 2), (y_chip, 2), (y_final, 1), (project, 3), (pass_on, 0),
                (y_chip, 3), (y_final, 2), (pass_on, 1), (y_final, 3), (pass_on, 2)]}
    for k in range(max(plan) + 1):
        if k < 2 * chunks:
            attend(k)
        if k == 1:
            arrive(n_copies)
        for stage, i in plan.get(k, ()):
            stage(i)
    for i in range(chunks):
        for c in ag[i] if i == chunks - 1 else ag[i][chips - 1:]:
            c.wait_recv()
    for c in q_copies + n_copies:
        c.wait_send()
    for i in range(chunks):
        for c in [od[i], yd[i]] + oi[i] + yi[i] + ag[i]:
            c.wait_send()


def write_kernel(which, k_in, new_ref, pos_ref, *refs):
    if which == 0:
        y_ref, k_out, k_ref, y_out, bsem, ysem = refs
        cy = pltpu.make_async_copy(y_ref, y_out, ysem)
    else:
        k_out, k_ref, bsem, ysem = refs
    batch, local_len = k_ref.shape[0], k_ref.shape[1] // 8
    base = lax.axis_index('seq') * local_len
    pieces = bsem.shape[0]
    pb = batch // pieces
    bulk = []
    for i in range(pieces):
        @pl.loop(i * pb, (i + 1) * pb)
        def _(b):
            rel = pos_ref[b] - base

            @pl.when((rel >= 0) & (rel < local_len))
            def _():
                k_ref[b, pl.ds(pl.multiple_of(rel * 8, 8), 8), :] = new_ref[which, pl.ds(pl.multiple_of(b * 8, 8), 8), :]
        part = pl.ds(i * pb, pb)
        c = pltpu.make_async_copy(k_ref.at[part], k_out.at[part], bsem.at[i])
        c.start()
        bulk.append(c)
    if which == 0:
        cy.start()
        bulk.append(cy)
    for c in bulk:
        c.wait()


def solution(mesh):
    cache_spec = P('rep', 'seq', None, None)
    in_specs = (P('rep', None), P(), P(), P(), P('seq', None), cache_spec, cache_spec, P('rep'))
    out_specs = (P('rep', None), cache_spec, cache_spec)
    chips = mesh.shape['seq'] // CORES
    assert chips == 4
    vm = pl.BlockSpec(memory_space=pltpu.VMEM)
    hbm = pl.BlockSpec(memory_space=pl.ANY)
    sm = pl.BlockSpec(memory_space=pltpu.SMEM)

    def local_step(x, wq, wk, wv, wo, k, v, pos):
        shape4 = k.shape
        batch, width = x.shape
        k3 = k.reshape(batch, -1, k.shape[-1])
        v3 = v.reshape(k3.shape)
        chunks = 4
        cb = batch // chunks
        dma = pltpu.SemaphoreType.DMA
        in_hbm = lambda a: pltpu.with_memory_space_constraint(a, pltpu.HBM)
        in_vmem = lambda a: pltpu.with_memory_space_constraint(a, pltpu.VMEM)
        y, ko, vo, new = pl.pallas_call(
            functools.partial(step_kernel, chips),
            out_shape=(pltpu.VMEM((batch, wo.shape[1]), BF16), pltpu.VMEM(k3.shape, BF16), pltpu.VMEM(k3.shape, BF16),
                       pltpu.VMEM((2, batch * 8, 128), BF16)),
            in_specs=[hbm] * 7 + [sm],
            out_specs=[vm] * 4,
            scratch_shapes=[
                pltpu.VMEM((batch, width), BF16), pltpu.VMEM((3, width, 512), BF16), pltpu.VMEM(wo.shape, BF16),
                pltpu.VMEM((batch * 8, 128), F32), pltpu.VMEM((4, batch * 8, 128), BF16), pltpu.VMEM((4, batch * 4, 128), BF16), pltpu.VMEM((k3.shape[1], 128), F32), pltpu.VMEM((k3.shape[1], 128), F32), pltpu.VMEM((2, 8, 128), F32), pltpu.VMEM((2, batch), jnp.int32),
                pltpu.VMEM((4, cb * 8, 128), F32), pltpu.VMEM((4, cb * 8, 128), F32), pltpu.VMEM((4, cb * 8, 128), F32),
                pltpu.VMEM((chunks, CORES, 4, cb * 4 + 16, 128), F32), pltpu.VMEM((chunks, 4, cb * 4 + 16, 128), F32),
                pltpu.VMEM((chunks, chips - 1, cb * 4 + 16, 128), F32),
                pltpu.VMEM((chunks, CORES, 4, cb, 512), F32), pltpu.VMEM((chunks, 4, cb, 512), F32), pltpu.VMEM((chunks, chips - 1, cb, 512), F32),
                dma((8,)), dma((2, chunks)), dma((5,)), dma((5,)), dma((5,)), dma((5,)), dma((chunks,)), dma((chunks,)),
                dma((chunks, chips - 1)), dma((chunks, chips - 1)), dma((chunks,)), dma((chunks,)),
                dma((chunks, chips - 1)), dma((chunks, chips - 1)), dma((chunks, chips * CORES - 1)), dma((chunks, chips * CORES - 1))],
            compiler_params=pltpu.CompilerParams(collective_id=0, has_side_effects=True, vmem_limit_bytes=29 << 20),
            name='step',
        )(in_hbm(x), in_hbm(wq), in_hbm(wk), in_hbm(wv), in_hbm(wo), in_hbm(k3), in_hbm(v3), pos)

        def write(which, cache, pieces, *extra):
            return pl.pallas_call(
                functools.partial(write_kernel, which),
                out_shape=(jax.ShapeDtypeStruct(k3.shape, BF16), pltpu.VMEM(k3.shape, BF16), *(jax.ShapeDtypeStruct(e.shape, BF16) for e in extra)),
                in_specs=[vm, vm, sm] + [vm] * len(extra),
                out_specs=[hbm, vm] + [hbm] * len(extra),
                scratch_shapes=[dma((pieces,)), dma],
                input_output_aliases={0: 1},
                compiler_params=pltpu.CompilerParams(vmem_limit_bytes=4 << 20),
                name='write',
            )(in_vmem(cache), in_vmem(new), pos, *(in_vmem(e) for e in extra))
        ko, _, y = write(0, ko, 16, y)
        vo, _ = write(1, vo, 16)
        return y, ko.reshape(shape4), vo.reshape(shape4)

    return jax.shard_map(local_step, mesh=mesh, in_specs=in_specs, out_specs=out_specs, check_vma=False)
```

profile of v0, /device:TPU:113, one launch (start us, length us, event | category | flops | bytes accessed | tf_op | source)
XLA Modules:
  0.0 59.8 jit_solution(10621935407921392496)
XLA Ops:
  0.6 0.0 copy-start
  0.6 45.7 %step.1 = (bf16[64,4096]{1,0:T(8,128)(2,1)S(1)}, bf16[64,1024,128]{2,1,0:T(8,128)(2,1)S(1)}, bf16[64,1024,128]{2,1,0:T(8,128)(2,1)S(1)}, bf16[2,512,128]{2,1,0:T(8,128)(2,1)S(1)}) custom-call(bf16[64,4096]{1,0:T(8,128)(2,1)} %x_hbm.1, bf16[4096,4096]{1,0:T(8,128)(2,1)} %wq_hbm.1, bf16[4096,1024]{1,0:T(8,128)(2,1)} %wk_hbm.1, bf16[4096,1024]{1,0:T(8,128)(2,1)} %wv_hbm.1, ...), custom_call_target="tpu_custom_call" | custom-call | tf_op jit(solution)/shard_map/step/pallas_call | solution.py:409
  46.4 0.0 copy-done
  46.4 6.7 %write.2 = (bf16[64,1024,128]{2,1,0:T(8,128)(2,1)}, bf16[64,1024,128]{2,1,0:T(8,128)(2,1)S(1)}, bf16[64,4096]{1,0:T(8,128)(2,1)}) custom-call(bf16[64,1024,128]{2,1,0:T(8,128)(2,1)S(1)} %get-tuple-element.10.k_in, bf16[2,512,128]{2,1,0:T(8,128)(2,1)S(1)} %get-tuple-element.11.new_ref, s32[64]{0:T(128)S(1)} %copy-done, ...), custom_call_target="tpu_custom_call", output_to_operand_aliasing={{1}: (0, {})} | custom-call | tf_op jit(solution)/shard_map/write/pallas_call | solution.py:430
  53.1 6.6 %write.3 = (bf16[64,1024,128]{2,1,0:T(8,128)(2,1)}, bf16[64,1024,128]{2,1,0:T(8,128)(2,1)S(1)}) custom-call(bf16[64,1024,128]{2,1,0:T(8,128)(2,1)S(1)} %get-tuple-element.15.k_in, bf16[2,512,128]{2,1,0:T(8,128)(2,1)S(1)} %get-tuple-element.11.new_ref, s32[64]{0:T(128)S(1)} %copy-done), custom_call_target="tpu_custom_call", output_to_operand_aliasing={{1}: (0, {})} | custom-call | tf_op jit(solution)/shard_map/write/pallas_call | solution.py:430
Async XLA Ops:
  0.6 45.7 %copy-start = (s32[64]{0:T(128)S(1)}, s32[64]{0:T(128)}, u32[]{:S(2)}) copy-start(s32[64]{0:T(128)} %pos_ref.5) | copy-start | bytes 772
where the time goes:
time: 59.9 us; the launch traced here: 59.8 us
  Pallas kernels  59 us (98%)
  between operations  0.83 us (1%)
    pallas_call x1, Pallas kernels, local_step(): pl.pallas_call(functools.partial(step_kernel, chips), out_shape=(pltpu.VM...  45.7 us
    pallas_call x2, Pallas kernels, write(): pl.pallas_call(functools.partial(write_kernel, which), out_shape=(jax.Sha...  13.3 us

commit v1 on v0

--- a/solution.py
+++ b/solution.py
@@ -337,7 +337,7 @@
 
     plan = {1: [(finalize, 0)], 2: [(chip_reduce, 0)], 3: [(finalize, 1)], 4: [(chip_reduce, 1)],
             5: [(finalize, 2), (project, 0)], 6: [(chip_reduce, 2), (y_chip, 0), (project, 1)],
-            7: [(finalize, 3), (y_chip, 1), (chip_reduce, 3), (y_final, 0), (project, 2), (y_chip, 2), (y_final, 1), (project, 3), (pass_on, 0),
+            7: [(finalize, 3), (chip_reduce, 3), (y_chip, 1), (y_final, 0), (project, 2), (y_chip, 2), (y_final, 1), (project, 3), (pass_on, 0),
                 (y_chip, 3), (y_final, 2), (pass_on, 1), (y_final, 3), (pass_on, 2)]}
     for k in range(max(plan) + 1):
         if k < 2 * chunks:
@@ -356,33 +356,32 @@
             c.wait_send()
 
 
-def write_kernel(which, k_in, new_ref, pos_ref, *refs):
-    if which == 0:
-        y_ref, k_out, k_ref, y_out, bsem, ysem = refs
-        cy = pltpu.make_async_copy(y_ref, y_out, ysem)
-    else:
-        k_out, k_ref, bsem, ysem = refs
+def write_kernel(k_in, v_in, new_ref, pos_ref, y_ref, k_out, k_ref, v_ref, y_out, bsem, ysem):
     batch, local_len = k_ref.shape[0], k_ref.shape[1] // 8
     base = lax.axis_index('seq') * local_len
     pieces = bsem.shape[0]
     pb = batch // pieces
-    bulk = []
-    for i in range(pieces):
-        @pl.loop(i * pb, (i + 1) * pb)
+    cy = pltpu.make_async_copy(y_ref, y_out, ysem)
+
+    def patch(cache, which, first, last):
+        @pl.loop(first, last)
         def _(b):
             rel = pos_ref[b] - base
 
             @pl.when((rel >= 0) & (rel < local_len))
             def _():
-                k_ref[b, pl.ds(pl.multiple_of(rel * 8, 8), 8), :] = new_ref[which, pl.ds(pl.multiple_of(b * 8, 8), 8), :]
+                cache[b, pl.ds(pl.multiple_of(rel * 8, 8), 8), :] = new_ref[which, pl.ds(pl.multiple_of(b * 8, 8), 8), :]
+
+    copies = []
+    for i in range(pieces):
+        patch(k_ref, 0, i * pb, (i + 1) * pb)
         part = pl.ds(i * pb, pb)
         c = pltpu.make_async_copy(k_ref.at[part], k_out.at[part], bsem.at[i])
         c.start()
-        bulk.append(c)
-    if which == 0:
-        cy.start()
-        bulk.append(cy)
-    for c in bulk:
+        copies.append(c)
+    cy.start()
+    patch(v_ref, 1, 0, batch)
+    for c in copies + [cy]:
         c.wait()
 
 
@@ -426,19 +425,17 @@
             name='step',
         )(in_hbm(x), in_hbm(wq), in_hbm(wk), in_hbm(wv), in_hbm(wo), in_hbm(k3), in_hbm(v3), pos)
 
-        def write(which, cache, pieces, *extra):
-            return pl.pallas_call(
-                functools.partial(write_kernel, which),
-                out_shape=(jax.ShapeDtypeStruct(k3.shape, BF16), pltpu.VMEM(k3.shape, BF16), *(jax.ShapeDtypeStruct(e.shape, BF16) for e in extra)),
-                in_specs=[vm, vm, sm] + [vm] * len(extra),
-                out_specs=[hbm, vm] + [hbm] * len(extra),
-                scratch_shapes=[dma((pieces,)), dma],
-                input_output_aliases={0: 1},
-                compiler_params=pltpu.CompilerParams(vmem_limit_bytes=4 << 20),
-                name='write',
-            )(in_vmem(cache), in_vmem(new), pos, *(in_vmem(e) for e in extra))
-        ko, _, y = write(0, ko, 16, y)
-        vo, _ = write(1, vo, 16)
+        pieces = 16
+        ko, _, vo, y = pl.pallas_call(
+            write_kernel,
+            out_shape=(jax.ShapeDtypeStruct(k3.shape, BF16), pltpu.VMEM(k3.shape, BF16), pltpu.VMEM(k3.shape, BF16), jax.ShapeDtypeStruct(y.shape, BF16)),
+            in_specs=[vm, vm, vm, sm, vm],
+            out_specs=[hbm, vm, vm, hbm],
+            scratch_shapes=[dma((pieces,)), dma],
+            input_output_aliases={0: 1, 1: 2},
+            compiler_params=pltpu.CompilerParams(vmem_limit_bytes=4 << 20),
+            name='write',
+        )(in_vmem(ko), in_vmem(vo), in_vmem(new), pos, in_vmem(y))
         return y, ko.reshape(shape4), vo.reshape(shape4)
 
     return jax.shard_map(local_step, mesh=mesh, in_specs=in_specs, out_specs=out_specs, check_vma=False)

time: 59.9 us -> 60.8 us (1.015)
  local copies, waits for them, and re-layouts: 0.01 us -> 6.17 us
  Pallas kernels: 59 us -> 53.9 us
    pallas_call x2 -> x1, Pallas kernels: 13.3 us -> 6.71 us  [local_step(): pl.pallas_call(write_kernel, out_shape=(jax.ShapeDtypeStruct(k3.shape, BF...]
    unnamed x2 -> x3, local copies, waits for them, and re-layouts: 0.01 us -> 6.17 us
    pallas_call x1, Pallas kernels: 45.7 us -> 47.2 us  [local_step(): pl.pallas_call(functools.partial(step_kernel, chips), out_shape=(pltpu.VM...]
where the time goes in v1:
time: 60.8 us; the launch traced here: 60.7 us
  Pallas kernels  53.9 us (89%)
  local copies, waits for them, and re-layouts  6.17 us (10%)
  between operations  0.67 us (1%)
    pallas_call x1, Pallas kernels, local_step(): pl.pallas_call(functools.partial(step_kernel, chips), out_shape=(pltpu.VM...  47.2 us
    pallas_call x1, Pallas kernels, local_step(): pl.pallas_call(write_kernel, out_shape=(jax.ShapeDtypeStruct(k3.shape, BF...  6.71 us
    unnamed x3, local copies, waits for them, and re-layouts  6.17 us

profile of v1, /device:TPU:113, one launch (start us, length us, event | category | flops | bytes accessed | tf_op | source)
XLA Modules:
  0.0 60.7 jit_solution(12104155354093895508)
XLA Ops:
  0.6 0.0 copy-start
  0.6 47.2 %step.1 = (bf16[64,4096]{1,0:T(8,128)(2,1)S(1)}, bf16[64,1024,128]{2,1,0:T(8,128)(2,1)S(1)}, bf16[64,1024,128]{2,1,0:T(8,128)(2,1)S(1)}, bf16[2,512,128]{2,1,0:T(8,128)(2,1)S(1)}) custom-call(bf16[64,4096]{1,0:T(8,128)(2,1)} %x_hbm.1, bf16[4096,4096]{1,0:T(8,128)(2,1)} %wq_hbm.1, bf16[4096,1024]{1,0:T(8,128)(2,1)} %wk_hbm.1, bf16[4096,1024]{1,0:T(8,128)(2,1)} %wv_hbm.1, ...), custom_call_target="tpu_custom_call" | custom-call | tf_op jit(solution)/shard_map/step/pallas_call | solution.py:408
  47.8 0.0 copy-done
  47.8 6.7 %write.1 = (bf16[64,1024,128]{2,1,0:T(8,128)(2,1)}, bf16[64,1024,128]{2,1,0:T(8,128)(2,1)S(1)}, bf16[64,1024,128]{2,1,0:T(8,128)(2,1)S(1)}, bf16[64,4096]{1,0:T(8,128)(2,1)}) custom-call(bf16[64,1024,128]{2,1,0:T(8,128)(2,1)S(1)} %get-tuple-element.10.k_in, ...), custom_call_target="tpu_custom_call", output_to_operand_aliasing={{1}: (0, {}), {2}: (1, {})} | custom-call | tf_op jit(solution)/shard_map/write/pallas_call | solution.py:429
  54.6 6.2 %copy.16 = bf16[64,128,8,128]{3,2,1,0:T(8,128)(2,1)} copy(bf16[64,128,8,128]{3,2,1,0:T(8,128)(2,1)S(1)} %bitcast.4) | data formatting | bytes 33554432
Async XLA Ops:
  0.6 47.2 %copy-start = (s32[64]{0:T(128)S(1)}, s32[64]{0:T(128)}, u32[]{:S(2)}) copy-start(s32[64]{0:T(128)} %pos_ref.3) | copy-start | bytes 772

commit v2 on v1

--- a/solution.py
+++ b/solution.py
@@ -337,7 +337,7 @@
 
     plan = {1: [(finalize, 0)], 2: [(chip_reduce, 0)], 3: [(finalize, 1)], 4: [(chip_reduce, 1)],
             5: [(finalize, 2), (project, 0)], 6: [(chip_reduce, 2), (y_chip, 0), (project, 1)],
-            7: [(finalize, 3), (chip_reduce, 3), (y_chip, 1), (y_final, 0), (project, 2), (y_chip, 2), (y_final, 1), (project, 3), (pass_on, 0),
+            7: [(finalize, 3), (y_chip, 1), (chip_reduce, 3), (y_final, 0), (project, 2), (y_chip, 2), (y_final, 1), (project, 3), (pass_on, 0),
                 (y_chip, 3), (y_final, 2), (pass_on, 1), (y_final, 3), (pass_on, 2)]}
     for k in range(max(plan) + 1):
         if k < 2 * chunks:

time: 60.8 us -> 59.3 us (0.975)
  Pallas kernels: 53.9 us -> 52.4 us
    pallas_call x1, Pallas kernels: 47.2 us -> 45.7 us  [local_step(): pl.pallas_call(functools.partial(step_kernel, chips), out_shape=(pltpu.VM...]
where the time goes in v2:
time: 59.3 us
  Pallas kernels  52.4 us (88%)
  local copies, waits for them, and re-layouts  6.17 us (10%)
  between operations  0.67 us (1%)
    pallas_call x1, Pallas kernels, local_step(): pl.pallas_call(functools.partial(step_kernel, chips), out_shape=(pltpu.VM...  45.7 us
    pallas_call x1, Pallas kernels, local_step(): pl.pallas_call(write_kernel, out_shape=(jax.ShapeDtypeStruct(k3.shape, BF...  6.71 us
    unnamed x3, local copies, waits for them, and re-layouts  6.17 us

profile of v2, /device:TPU:113, one launch (start us, length us, event | category | flops | bytes accessed | tf_op | source)
XLA Modules:
  0.0 59.3 jit_solution(16145573118584717464)
XLA Ops:
  0.6 0.0 copy-start
  0.6 45.7 %step.1 = (bf16[64,4096]{1,0:T(8,128)(2,1)S(1)}, bf16[64,1024,128]{2,1,0:T(8,128)(2,1)S(1)}, bf16[64,1024,128]{2,1,0:T(8,128)(2,1)S(1)}, bf16[2,512,128]{2,1,0:T(8,128)(2,1)S(1)}) custom-call(bf16[64,4096]{1,0:T(8,128)(2,1)} %x_hbm.1, bf16[4096,4096]{1,0:T(8,128)(2,1)} %wq_hbm.1, bf16[4096,1024]{1,0:T(8,128)(2,1)} %wk_hbm.1, bf16[4096,1024]{1,0:T(8,128)(2,1)} %wv_hbm.1, ...), custom_call_target="tpu_custom_call" | custom-call | tf_op jit(solution)/shard_map/step/pallas_call | solution.py:408
  46.4 0.0 copy-done
  46.4 6.7 %write.1 = (bf16[64,1024,128]{2,1,0:T(8,128)(2,1)}, bf16[64,1024,128]{2,1,0:T(8,128)(2,1)S(1)}, bf16[64,1024,128]{2,1,0:T(8,128)(2,1)S(1)}, bf16[64,4096]{1,0:T(8,128)(2,1)}) custom-call(bf16[64,1024,128]{2,1,0:T(8,128)(2,1)S(1)} %get-tuple-element.10.k_in, ...), custom_call_target="tpu_custom_call", output_to_operand_aliasing={{1}: (0, {}), {2}: (1, {})} | custom-call | tf_op jit(solution)/shard_map/write/pallas_call | solution.py:429
  53.1 6.2 %copy.16 = bf16[64,128,8,128]{3,2,1,0:T(8,128)(2,1)} copy(bf16[64,128,8,128]{3,2,1,0:T(8,128)(2,1)S(1)} %bitcast.4) | data formatting | bytes 33554432
Async XLA Ops:
  0.6 45.7 %copy-start = (s32[64]{0:T(128)S(1)}, s32[64]{0:T(128)}, u32[]{:S(2)}) copy-start(s32[64]{0:T(128)} %pos_ref.3) | copy-start | bytes 772
